TPU v7x, 32 devices: a whole 2x2x4 slice. The times are simulated.
32 devices in a mesh: replica: 4 (over y, x), fsdp: 8 (over z, core).
Axes of the slice: x: 2, y: 2, z: 4, core: 2. Of those that a mesh axis runs over, the one named last changes fastest.
Arguments:
- base_weights: float32 [8192, 1024], P('fsdp'), may hold values from -5 to 5, as said below
- inner_weights: bfloat16 [4, 8192, 1024], P('replica', 'fsdp'), may hold values from -12 to 12, as said below
- momentum: float32 [8192, 1024], P(('fsdp', 'replica')), may hold values from -1 to 1
Outputs:
- new_base: float32 [8192, 1024], P('fsdp')
- new_momentum: float32 [8192, 1024], P(('fsdp', 'replica'))
- new_inner: bfloat16 [4, 8192, 1024], P('replica', 'fsdp')
Inputs may be any that keep to these rules, and one draw needn't show every extreme that they name: `base_weights`: the shared outer weights, multiples of 2 ** -16. `inner_weights`: each replica's weights after its inner steps, multiples of 2 ** -16.
All inputs are finite; a program needn't handle non-finite values.
Results may differ from a plain program's by a relative error of at most 0.0015.
Values may be sent and summed in bfloat16 or wider, within the bound.
A program may use at most 64 MiB of HBM per device.

v0:
```python
import functools

import jax
import jax.numpy as jnp
from jax import lax
from jax.experimental import pallas as pl
from jax.experimental.pallas import tpu as pltpu
from jax.sharding import PartitionSpec as P

BLOCK = 128
HALF_GROUPS = 4
EARLY_GROUPS = 2
ENCODE_ROWS = 256
PLAIN_ROWS = 128

code_limit = 448.0
outer_rate = 0.7
outer_momentum = 0.9
blend_share = 0.5
clip_rms = 0.02
epsilon = 1e-06

MESH = pl.DeviceIdType.MESH


def decoded_deltas(deltas):
    peaks = jnp.max(jnp.abs(deltas), axis=1, keepdims=True) + epsilon
    rough = peaks * (1.0 / code_limit)
    wide = rough * (2.0**23 + 1.0)
    power = wide - (wide - rough)
    scales = jnp.where(power * code_limit < peaks, power + power, power)
    nudged = deltas * (1.0 + 2.0**-23)
    wide_deltas = nudged * (2.0**20 + 1.0)
    four_bits = wide_deltas - (wide_deltas - nudged)
    shift = scales * (1.5 * 2.0**14)
    fixed_step = (nudged + shift) - shift
    return jnp.where(jnp.abs(deltas) < scales * 2.0**-6, fixed_step, four_bits)


def grid_sides(replicas):
    side = 1 << (replicas.bit_length() // 2)
    while replicas % side:
        side -= 1
    return side, replicas // side


def kernel(
    dims,
    base_hbm, inner_hbm, momentum_hbm,
    new_base, new_momentum, new_inner,
    base_v, inner_v, momentum_v, dec, first, second, grad, update, early,
    square_mine, square_near, square_row, square_far,
    load_sems, send_one, recv_one, send_two, recv_two, send_all, recv_all,
    near_send, near_recv, far_send, far_recv,
):
    replicas, shards_count, rows, columns, groups, total = dims
    width = columns // groups
    span_x, span_y = grid_sides(replicas)
    tile = min(PLAIN_ROWS, rows)
    encode_tile = min(ENCODE_ROWS, rows)
    me = lax.axis_index("replica")
    row_me = lax.axis_index("fsdp")
    me_x, me_y = lax.rem(me, span_x), me // span_x

    def spans(g):
        return (span_x, span_y) if g % 2 == 0 else (span_y, span_x)

    def owner(g, dp, dq):
        dx, dy = (dp, dq) if g % 2 == 0 else (dq, dp)
        return lax.rem(me_y + dy, span_y) * span_x + lax.rem(me_x + dx, span_x)

    def near(step):
        return lax.rem(me + step, replicas)

    def far(step):
        return lax.rem(row_me + step, shards_count)

    def row_start(index):
        return pl.multiple_of(index * rows, rows)

    barrier = pltpu.get_barrier_semaphore()
    for step in range(1, replicas):
        pl.semaphore_signal(barrier, inc=1, device_id={"replica": near(step)}, device_id_type=MESH)
    for step in range(1, shards_count):
        pl.semaphore_signal(barrier, inc=1, device_id={"fsdp": far(step)}, device_id_type=MESH)

    load_order = [(dx, dy) for dy in reversed(range(span_y)) for dx in reversed(range(span_x))]
    loads = []
    for at, (dx, dy) in enumerate(load_order):
        here = pl.ds(row_start(owner(0, dx, dy)), rows)
        pair = (
            pltpu.make_async_copy(base_hbm.at[here], base_v.at[here], load_sems.at[at, 0]),
            pltpu.make_async_copy(inner_hbm.at[0, here], inner_v.at[here], load_sems.at[at, 1]),
        )
        for copy in pair:
            copy.start()
        loads.append(pair)
    momentum_load = pltpu.make_async_copy(momentum_hbm, momentum_v, load_sems.at[replicas, 0])
    momentum_load.start()

    def encode(g, dp, dq):
        slot = dp * spans(g)[1] + dq
        start = row_start(owner(g, dp, dq))

        @pl.loop(0, rows // encode_tile)
        def _(t):
            at = pl.ds(pl.multiple_of(start + t * encode_tile, encode_tile), encode_tile)
            to = pl.ds(pl.multiple_of(t * encode_tile, encode_tile), encode_tile)
            for c in range(0, width, BLOCK):
                cols = pl.ds(g * width + c, BLOCK)
                deltas = base_v[at, cols] - inner_v[at, cols].astype(jnp.float32)
                dec[g, slot, to, pl.ds(c, BLOCK)] = decoded_deltas(deltas).astype(jnp.bfloat16)

    def copy_one(g, dp, dq):
        slot = dp * spans(g)[1] + dq
        return pltpu.make_async_remote_copy(
            src_ref=dec.at[g, slot], dst_ref=first.at[g, slot],
            send_sem=send_one.at[g, slot], recv_sem=recv_one.at[g, slot],
            device_id={"replica": owner(g, dp, 0)}, device_id_type=MESH,
        )

    def copy_two(g, dq):
        return pltpu.make_async_remote_copy(
            src_ref=dec.at[g, dq], dst_ref=second.at[g, dq],
            send_sem=send_two.at[g, dq], recv_sem=recv_two.at[g, dq],
            device_id={"replica": owner(g, 0, dq)}, device_id_type=MESH,
        )

    def copy_all(g, dp, dq, source):
        np, nq = spans(g)
        slot = ((np - dp) % np) * nq + (source if dp else (nq - dq) % nq)
        blocks = early if g < EARLY_GROUPS else update
        return pltpu.make_async_remote_copy(
            src_ref=blocks.at[g, source if dp else 0], dst_ref=blocks.at[g, slot],
            send_sem=send_all.at[g, slot], recv_sem=recv_all.at[g, slot],
            device_id={"replica": owner(g, dp, dq)}, device_id_type=MESH,
        )

    waited = set()

    def await_load(g, dp, dq):
        key = (dp, dq) if g % 2 == 0 else (dq, dp)
        if key not in waited:
            waited.add(key)
            for copy in loads[load_order.index(key)]:
                copy.wait()

    sends = []
    greeted = False
    most = max(span_x, span_y)
    for dq in reversed(range(most)):
        for dp in reversed(range(1, most)):
            for g in range(groups):
                np, nq = spans(g)
                if dp < np and dq < nq:
                    await_load(g, dp, dq)
                    encode(g, dp, dq)
                    if not greeted:
                        pl.semaphore_wait(barrier, replicas - 1 + shards_count - 1)
                        greeted = True
                    copy = copy_one(g, dp, dq)
                    copy.start()
                    sends.append(copy)
    for dq in reversed(range(most)):
        for g in range(groups):
            if dq < spans(g)[1]:
                await_load(g, 0, dq)
                encode(g, 0, dq)

    for dq in reversed(range(most)):
        for g in range(groups):
            np, nq = spans(g)
            if dq >= nq:
                continue
            for dp in range(1, np):
                copy_one(g, dp, dq).wait_recv()

            @pl.loop(0, rows // tile)
            def _(t):
                at = pl.ds(pl.multiple_of(t * tile, tile), tile)
                summed = dec[g, dq, at].astype(jnp.float32)
                for dp in range(1, np):
                    summed += first[g, dp * nq + dq, at].astype(jnp.float32)
                if dq:
                    dec[g, dq, at] = summed.astype(jnp.bfloat16)
                else:
                    grad[at, pl.ds(g * width, width)] = summed

            if dq:
                copy = copy_two(g, dq)
                copy.start()
                sends.append(copy)

    squares = jnp.zeros((8, BLOCK), jnp.float32)
    for g in range(groups):
        nq = spans(g)[1]
        for dq in range(1, nq):
            copy_two(g, dq).wait_recv()

        def add(t, squares):
            at = pl.ds(pl.multiple_of(t * tile, tile), tile)
            for c in range(0, width, BLOCK):
                cols = pl.ds(g * width + c, BLOCK)
                summed = grad[at, cols]
                for dq in range(1, nq):
                    summed += second[g, dq, at, pl.ds(c, BLOCK)].astype(jnp.float32)
                outer = summed * (1.0 / replicas)
                grad[at, cols] = outer
                square = outer * outer
                for s in range(0, tile, 8):
                    squares += square[s : s + 8]
            return squares

        squares = lax.fori_loop(0, rows // tile, add, squares)

    square_mine[...] = squares
    square_near[0] = squares
    near_copies = []
    for step in range(1, replicas):
        copy = pltpu.make_async_remote_copy(
            src_ref=square_mine, dst_ref=square_near.at[step],
            send_sem=near_send.at[step], recv_sem=near_recv.at[step],
            device_id={"replica": near(step)}, device_id_type=MESH,
        )
        copy.start()
        near_copies.append(copy)
    sends += near_copies

    momentum_load.wait()
    for g in range(EARLY_GROUPS):
        @pl.loop(0, rows // tile)
        def _(t):
            at = pl.ds(pl.multiple_of(t * tile, tile), tile)
            cols = pl.ds(g * width, width)
            early[g, 0, 0, at] = grad[at, cols].astype(jnp.bfloat16)
            early[g, 0, 1, at] = momentum_v[at, cols].astype(jnp.bfloat16)

        for dq in range(1, spans(g)[1]):
            copy = copy_all(g, 0, dq, 0)
            copy.start()
            sends.append(copy)
    for g in range(EARLY_GROUPS):
        for dp in range(1, spans(g)[0]):
            copy = copy_all(g, dp, 0, 0)
            copy.start()
            sends.append(copy)

    for copy in near_copies:
        copy.wait_recv()
    squares = square_near[me]
    for at in range(1, replicas):
        squares += square_near[lax.rem(me + replicas - at, replicas)]
    square_row[...] = squares
    square_far[0] = squares
    far_copies = []
    for step in range(1, shards_count):
        copy = pltpu.make_async_remote_copy(
            src_ref=square_row, dst_ref=square_far.at[step],
            send_sem=far_send.at[step], recv_sem=far_recv.at[step],
            device_id={"fsdp": far(step)}, device_id_type=MESH,
        )
        copy.start()
        far_copies.append(copy)
    sends += far_copies

    def pass_on(g):
        np, nq = spans(g)
        for dq in range(1, nq):
            copy_all(g, 0, (nq - dq) % nq, 0).wait_recv()
            for dp in range(1, np):
                copy = copy_all(g, dp, 0, dq)
                copy.start()
                sends.append(copy)

    for g in range(EARLY_GROUPS):
        pass_on(g)
    for copy in far_copies:
        copy.wait_recv()
    squares = square_far[row_me]
    for at in range(1, shards_count):
        squares += square_far[lax.rem(row_me + shards_count - at, shards_count)]
    mean_square = jnp.full((1, BLOCK), jnp.sum(squares), jnp.float32) / total
    clip_factor = jnp.minimum(1.0, clip_rms / jnp.sqrt(mean_square + epsilon))

    def moved_and_change(outer, kept):
        step_term = clip_factor * outer
        moved = outer_momentum * kept + step_term
        return moved, step_term + outer_momentum * moved

    def advance(g):
        @pl.loop(0, rows // tile)
        def _(t):
            at = pl.ds(pl.multiple_of(t * tile, tile), tile)
            for c in range(0, width, BLOCK):
                cols = pl.ds(g * width + c, BLOCK)
                moved, change = moved_and_change(grad[at, cols], momentum_v[at, cols])
                new_momentum[at, cols] = moved
                if g >= EARLY_GROUPS:
                    update[g, 0, at, pl.ds(c, BLOCK)] = change.astype(jnp.bfloat16)

    for g in range(EARLY_GROUPS, groups):
        advance(g)
        for dq in range(1, spans(g)[1]):
            copy = copy_all(g, 0, dq, 0)
            copy.start()
            sends.append(copy)
    for g in range(EARLY_GROUPS, groups):
        for dp in range(1, spans(g)[0]):
            copy = copy_all(g, dp, 0, 0)
            copy.start()
            sends.append(copy)

    def finish(g, dp, dq):
        slot = dp * spans(g)[1] + dq
        start = row_start(owner(g, dp, dq))

        @pl.loop(0, rows // tile)
        def _(t):
            at = pl.ds(pl.multiple_of(start + t * tile, tile), tile)
            to = pl.ds(pl.multiple_of(t * tile, tile), tile)
            for c in range(0, width, BLOCK):
                cols = pl.ds(g * width + c, BLOCK)
                from_cols = pl.ds(c, BLOCK)
                if g < EARLY_GROUPS:
                    _, change = moved_and_change(
                        early[g, slot, 0, to, from_cols].astype(jnp.float32),
                        early[g, slot, 1, to, from_cols].astype(jnp.float32),
                    )
                else:
                    change = update[g, slot, to, from_cols].astype(jnp.float32)
                fresh = base_v[at, cols] - outer_rate * change
                new_base[at, cols] = fresh
                blended = blend_share * inner_v[at, cols].astype(jnp.float32) + (
                    1.0 - blend_share
                ) * fresh
                new_inner[0, at, cols] = blended.astype(jnp.bfloat16)

    def finish_last(g, dq):
        np = spans(g)[0]
        for dp in range(1, np):
            copy_all(g, (np - dp) % np, 0, dq).wait_recv()
            finish(g, dp, dq)

    for g in range(EARLY_GROUPS):
        advance(g)
        for dq in range(spans(g)[1]):
            finish(g, 0, dq)
    for g in range(EARLY_GROUPS, groups):
        finish(g, 0, 0)
    for g in range(EARLY_GROUPS, groups):
        pass_on(g)
    for g in range(EARLY_GROUPS, groups):
        for dq in range(1, spans(g)[1]):
            finish(g, 0, dq)
    for dq in range(most):
        for g in range(groups):
            if dq < spans(g)[1]:
                finish_last(g, dq)
    for copy in sends:
        copy.wait_send()


def write_out(*refs):
    sems = refs[-1]
    parts = len(refs) // 2
    copies = [
        pltpu.make_async_copy(refs[i], refs[parts + i], sems.at[i]) for i in range(parts)
    ]
    for copy in copies:
        copy.start()
    for copy in copies:
        copy.wait()


def shards(base_weights, inner_weights, momentum):
    replicas = lax.axis_size("replica")
    shards_count = lax.axis_size("fsdp")
    local_rows, columns = base_weights.shape
    rows = local_rows // replicas
    groups = 2 * HALF_GROUPS
    width = columns // groups
    total = float(local_rows * shards_count * columns)
    dims = (replicas, shards_count, rows, columns, groups, total)
    most = max(grid_sides(replicas))
    dma = pltpu.SemaphoreType.DMA
    blocks = (groups, replicas, rows, width)
    outside = pl.BlockSpec(memory_space=pltpu.HBM)
    vmem = pl.BlockSpec(memory_space=pltpu.VMEM)
    in_hbm = functools.partial(pltpu.with_memory_space_constraint, memory_space=pltpu.HBM)
    in_vmem = functools.partial(pltpu.with_memory_space_constraint, memory_space=pltpu.VMEM)
    held = pl.pallas_call(
        functools.partial(kernel, dims),
        out_shape=(
            pltpu.VMEM(base_weights.shape, jnp.float32),
            pltpu.VMEM(momentum.shape, jnp.float32),
            pltpu.VMEM(inner_weights.shape, jnp.bfloat16),
        ),
        in_specs=[outside] * 3,
        out_specs=(vmem, vmem, vmem),
        scratch_shapes=[
            pltpu.VMEM((local_rows, columns), jnp.float32),
            pltpu.VMEM((local_rows, columns), jnp.bfloat16),
            pltpu.VMEM((rows, columns), jnp.float32),
            pltpu.VMEM(blocks, jnp.bfloat16),
            pltpu.VMEM(blocks, jnp.bfloat16),
            pltpu.VMEM((groups, most, rows, width), jnp.bfloat16),
            pltpu.VMEM((rows, columns), jnp.float32),
            pltpu.VMEM(blocks, jnp.bfloat16),
            pltpu.VMEM((max(EARLY_GROUPS, 1), replicas, 2, rows, width), jnp.bfloat16),
            pltpu.VMEM((8, BLOCK), jnp.float32),
            pltpu.VMEM((replicas, 8, BLOCK), jnp.float32),
            pltpu.VMEM((8, BLOCK), jnp.float32),
            pltpu.VMEM((shards_count, 8, BLOCK), jnp.float32),
            dma((replicas + 1, 2)),
            dma((groups, replicas)),
            dma((groups, replicas)),
            dma((groups, most)),
            dma((groups, most)),
            dma((groups, replicas)),
            dma((groups, replicas)),
            dma((replicas,)),
            dma((replicas,)),
            dma((shards_count,)),
            dma((shards_count,)),
        ],
        compiler_params=pltpu.CompilerParams(collective_id=0, has_side_effects=True, vmem_limit_bytes=36 * 2**20),
    )(in_hbm(base_weights), in_hbm(inner_weights), in_hbm(momentum))
    return pl.pallas_call(
        write_out,
        out_shape=tuple(jax.ShapeDtypeStruct(part.shape, part.dtype) for part in held),
        in_specs=[vmem] * len(held),
        out_specs=tuple(outside for part in held),
        scratch_shapes=[dma((len(held),))],
        compiler_params=pltpu.CompilerParams(vmem_limit_bytes=2**20),
    )(*[in_vmem(part) for part in held])


def solution(mesh):
    placed = (P("fsdp", None), P("replica", "fsdp", None), P(("fsdp", "replica"), None))
    return jax.shard_map(
        shards,
        mesh=mesh,
        in_specs=placed,
        out_specs=(P("fsdp", None), P(("fsdp", "replica"), None), P("replica", "fsdp", None)),
        check_vma=False,
    )
```

profile of v0, /device:TPU:0, one launch (start us, length us, event | category | flops | bytes accessed | tf_op | source)
XLA Modules:
  0.0 53.5 jit_solution(8661009172716560218)
XLA Ops:
  0.6 49.8 %shard_map.58 = (f32[1024,1024]{1,0:T(8,128)S(1)}, f32[256,1024]{1,0:T(8,128)S(1)}, bf16[1,1024,1024]{2,1,0:T(8,128)(2,1)S(1)}) custom-call(f32[1024,1024]{1,0:T(8,128)} %base_hbm.1, bf16[1,1024,1024]{2,1,0:T(8,128)(2,1)} %inner_hbm.1, f32[256,1024]{1,0:T(8,128)} %momentum_hbm.1), custom_call_target="tpu_custom_call" | custom-call | tf_op jit(solution)/shard_map/pallas_call | solution.py:391
  50.5 3.0 %shard_map.59 = (f32[1024,1024]{1,0:T(8,128)}, f32[256,1024]{1,0:T(8,128)}, bf16[1,1024,1024]{2,1,0:T(8,128)(2,1)}) custom-call(f32[1024,1024]{1,0:T(8,128)S(1)} %get-tuple-element.6.refs_0_, f32[256,1024]{1,0:T(8,128)S(1)} %get-tuple-element.7.refs_1_, bf16[1,1024,1024]{2,1,0:T(8,128)(2,1)S(1)} %get-tuple-element.8.refs_2_), custom_call_target="tpu_custom_call" | custom-call | tf_op jit(solution)/shard_map/pallas_call | solution.py:428
where the time goes:
time: 53.7 us; the launch traced here: 53.5 us
  Pallas kernels  52.9 us (99%)
  between operations  0.64 us (1%)
    pallas_call x1, Pallas kernels, shards(): pl.pallas_call(functools.partial(kernel, dims), out_shape=(pltpu.VMEM(bas...  49.8 us
    pallas_call x1, Pallas kernels, shards(): pl.pallas_call(write_out, out_shape=tuple((jax.ShapeDtypeStruct(part.shap...  3.04 us

commit v1 on v0

--- a/solution.py
+++ b/solution.py
@@ -37,6 +37,10 @@
     return jnp.where(jnp.abs(deltas) < scales * 2.0**-6, fixed_step, four_bits)
 
 
+def arrived(blocks, sem):
+    pltpu.make_async_copy(blocks, blocks, sem).wait()
+
+
 def grid_sides(replicas):
     side = 1 << (replicas.bit_length() // 2)
     while replicas % side:
@@ -50,8 +54,7 @@
     new_base, new_momentum, new_inner,
     base_v, inner_v, momentum_v, dec, first, second, grad, update, early,
     square_mine, square_near, square_row, square_far,
-    load_sems, send_one, recv_one, send_two, recv_two, send_all, recv_all,
-    near_send, near_recv, far_send, far_recv,
+    load_sems, send_sems, recv_sems, early_sems, square_sems, entry_sems,
 ):
     replicas, shards_count, rows, columns, groups, total = dims
     width = columns // groups
@@ -115,24 +118,34 @@
         slot = dp * spans(g)[1] + dq
         return pltpu.make_async_remote_copy(
             src_ref=dec.at[g, slot], dst_ref=first.at[g, slot],
-            send_sem=send_one.at[g, slot], recv_sem=recv_one.at[g, slot],
+            send_sem=send_sems.at[0], recv_sem=recv_sems.at[g, slot - 1],
             device_id={"replica": owner(g, dp, 0)}, device_id_type=MESH,
         )
 
     def copy_two(g, dq):
         return pltpu.make_async_remote_copy(
             src_ref=dec.at[g, dq], dst_ref=second.at[g, dq],
-            send_sem=send_two.at[g, dq], recv_sem=recv_two.at[g, dq],
+            send_sem=send_sems.at[0], recv_sem=recv_sems.at[g, dq - 1],
             device_id={"replica": owner(g, 0, dq)}, device_id_type=MESH,
         )
 
+    def arrival(g, dp, dq, source):
+        np, nq = spans(g)
+        return ((np - dp) % np) * nq + (source if dp else (nq - dq) % nq)
+
     def copy_all(g, dp, dq, source):
-        np, nq = spans(g)
-        slot = ((np - dp) % np) * nq + (source if dp else (nq - dq) % nq)
-        blocks = early if g < EARLY_GROUPS else update
+        slot = arrival(g, dp, dq, source)
         return pltpu.make_async_remote_copy(
-            src_ref=blocks.at[g, source if dp else 0], dst_ref=blocks.at[g, slot],
-            send_sem=send_all.at[g, slot], recv_sem=recv_all.at[g, slot],
+            src_ref=update.at[g, source if dp else 0], dst_ref=update.at[g, slot],
+            send_sem=send_sems.at[1], recv_sem=recv_sems.at[g, slot - 1],
+            device_id={"replica": owner(g, dp, dq)}, device_id_type=MESH,
+        )
+
+    def copy_early(g, part, dp, dq, source):
+        slot = arrival(g, dp, dq, source)
+        return pltpu.make_async_remote_copy(
+            src_ref=early.at[g, part, source if dp else 0], dst_ref=early.at[g, part, slot],
+            send_sem=send_sems.at[2], recv_sem=early_sems.at[g, part, slot - 1],
             device_id={"replica": owner(g, dp, dq)}, device_id_type=MESH,
         )
 
@@ -145,7 +158,6 @@
             for copy in loads[load_order.index(key)]:
                 copy.wait()
 
-    sends = []
     greeted = False
     most = max(span_x, span_y)
     for dq in reversed(range(most)):
@@ -158,9 +170,7 @@
                     if not greeted:
                         pl.semaphore_wait(barrier, replicas - 1 + shards_count - 1)
                         greeted = True
-                    copy = copy_one(g, dp, dq)
-                    copy.start()
-                    sends.append(copy)
+                    copy_one(g, dp, dq).start()
     for dq in reversed(range(most)):
         for g in range(groups):
             if dq < spans(g)[1]:
@@ -187,12 +197,9 @@
                     grad[at, pl.ds(g * width, width)] = summed
 
             if dq:
-                copy = copy_two(g, dq)
-                copy.start()
-                sends.append(copy)
-
-    squares = jnp.zeros((8, BLOCK), jnp.float32)
-    for g in range(groups):
+                copy_two(g, dq).start()
+
+    def add_group(g, squares):
         nq = spans(g)[1]
         for dq in range(1, nq):
             copy_two(g, dq).wait_recv()
@@ -206,76 +213,83 @@
                     summed += second[g, dq, at, pl.ds(c, BLOCK)].astype(jnp.float32)
                 outer = summed * (1.0 / replicas)
                 grad[at, cols] = outer
+                if g < EARLY_GROUPS:
+                    early[g, 0, 0, at, pl.ds(c, BLOCK)] = outer.astype(jnp.bfloat16)
                 square = outer * outer
                 for s in range(0, tile, 8):
                     squares += square[s : s + 8]
             return squares
 
-        squares = lax.fori_loop(0, rows // tile, add, squares)
-
-    square_mine[...] = squares
-    square_near[0] = squares
-    near_copies = []
-    for step in range(1, replicas):
-        copy = pltpu.make_async_remote_copy(
-            src_ref=square_mine, dst_ref=square_near.at[step],
-            send_sem=near_send.at[step], recv_sem=near_recv.at[step],
-            device_id={"replica": near(step)}, device_id_type=MESH,
-        )
-        copy.start()
-        near_copies.append(copy)
-    sends += near_copies
+        return lax.fori_loop(0, rows // tile, add, squares)
+
+    def early_first(g, part):
+        for dq in range(1, spans(g)[1]):
+            copy_early(g, part, 0, dq, 0).start()
+
+    def early_second(g, part, source):
+        for dp in range(1, spans(g)[0]):
+            copy_early(g, part, dp, 0, source).start()
 
     momentum_load.wait()
     for g in range(EARLY_GROUPS):
         @pl.loop(0, rows // tile)
         def _(t):
             at = pl.ds(pl.multiple_of(t * tile, tile), tile)
-            cols = pl.ds(g * width, width)
-            early[g, 0, 0, at] = grad[at, cols].astype(jnp.bfloat16)
-            early[g, 0, 1, at] = momentum_v[at, cols].astype(jnp.bfloat16)
-
-        for dq in range(1, spans(g)[1]):
-            copy = copy_all(g, 0, dq, 0)
-            copy.start()
-            sends.append(copy)
-    for g in range(EARLY_GROUPS):
-        for dp in range(1, spans(g)[0]):
-            copy = copy_all(g, dp, 0, 0)
-            copy.start()
-            sends.append(copy)
-
-    for copy in near_copies:
-        copy.wait_recv()
+            early[g, 1, 0, at] = momentum_v[at, pl.ds(g * width, width)].astype(jnp.bfloat16)
+
+    ahead = (1,)
+    squares = jnp.zeros((8, BLOCK), jnp.float32)
+    for g in range(EARLY_GROUPS):
+        squares = add_group(g, squares)
+        for part in ahead:
+            early_first(g, part)
+    for g in range(EARLY_GROUPS, groups):
+        squares = add_group(g, squares)
+
+    square_mine[...] = squares
+    square_near[0] = squares
+    for step in range(1, replicas):
+        pltpu.make_async_remote_copy(
+            src_ref=square_mine, dst_ref=square_near.at[step],
+            send_sem=square_sems.at[0], recv_sem=square_sems.at[1],
+            device_id={"replica": near(step)}, device_id_type=MESH,
+        ).start()
+    for g in range(EARLY_GROUPS):
+        for part in (1, 0):
+            if part not in ahead:
+                early_first(g, part)
+    for g in range(EARLY_GROUPS):
+        for part in (1, 0):
+            early_second(g, part, 0)
+
+    arrived(square_near.at[pl.ds(1, replicas - 1)], square_sems.at[1])
     squares = square_near[me]
     for at in range(1, replicas):
         squares += square_near[lax.rem(me + replicas - at, replicas)]
     square_row[...] = squares
     square_far[0] = squares
-    far_copies = []
     for step in range(1, shards_count):
-        copy = pltpu.make_async_remote_copy(
+        pltpu.make_async_remote_copy(
             src_ref=square_row, dst_ref=square_far.at[step],
-            send_sem=far_send.at[step], recv_sem=far_recv.at[step],
+            send_sem=square_sems.at[2], recv_sem=square_sems.at[3],
             device_id={"fsdp": far(step)}, device_id_type=MESH,
-        )
-        copy.start()
-        far_copies.append(copy)
-    sends += far_copies
+        ).start()
+
+    for g in range(EARLY_GROUPS):
+        np, nq = spans(g)
+        for dq in range(1, nq):
+            for part in (1, 0):
+                copy_early(g, part, 0, (nq - dq) % nq, 0).wait_recv()
+                early_second(g, part, dq)
 
     def pass_on(g):
         np, nq = spans(g)
         for dq in range(1, nq):
             copy_all(g, 0, (nq - dq) % nq, 0).wait_recv()
             for dp in range(1, np):
-                copy = copy_all(g, dp, 0, dq)
-                copy.start()
-                sends.append(copy)
-
-    for g in range(EARLY_GROUPS):
-        pass_on(g)
-    for copy in far_copies:
-        copy.wait_recv()
+                copy_all(g, dp, 0, dq).start()
+
+    arrived(square_far.at[pl.ds(1, shards_count - 1)], square_sems.at[3])
     squares = square_far[row_me]
     for at in range(1, shards_count):
         squares += square_far[lax.rem(row_me + shards_count - at, shards_count)]
@@ -301,14 +315,10 @@
     for g in range(EARLY_GROUPS, groups):
         advance(g)
         for dq in range(1, spans(g)[1]):
-            copy = copy_all(g, 0, dq, 0)
-            copy.start()
-            sends.append(copy)
+            copy_all(g, 0, dq, 0).start()
     for g in range(EARLY_GROUPS, groups):
         for dp in range(1, spans(g)[0]):
-            copy = copy_all(g, dp, 0, 0)
-            copy.start()
-            sends.append(copy)
+            copy_all(g, dp, 0, 0).start()
 
     def finish(g, dp, dq):
         slot = dp * spans(g)[1] + dq
@@ -323,8 +333,8 @@
                 from_cols = pl.ds(c, BLOCK)
                 if g < EARLY_GROUPS:
                     _, change = moved_and_change(
-                        early[g, slot, 0, to, from_cols].astype(jnp.float32),
-                        early[g, slot, 1, to, from_cols].astype(jnp.float32),
+                        early[g, 0, slot, to, from_cols].astype(jnp.float32),
+                        early[g, 1, slot, to, from_cols].astype(jnp.float32),
                     )
                 else:
                     change = update[g, slot, to, from_cols].astype(jnp.float32)
@@ -338,7 +348,11 @@
     def finish_last(g, dq):
         np = spans(g)[0]
         for dp in range(1, np):
-            copy_all(g, (np - dp) % np, 0, dq).wait_recv()
+            if g < EARLY_GROUPS:
+                for part in range(2):
+                    copy_early(g, part, (np - dp) % np, 0, dq).wait_recv()
+            else:
+                copy_all(g, (np - dp) % np, 0, dq).wait_recv()
             finish(g, dp, dq)
 
     for g in range(EARLY_GROUPS):
@@ -356,8 +370,12 @@
         for g in range(groups):
             if dq < spans(g)[1]:
                 finish_last(g, dq)
-    for copy in sends:
-        copy.wait_send()
+    others = pl.ds(0, replicas - 1)
+    arrived(dec.at[:, others], send_sems.at[0])
+    arrived(update.at[pl.ds(0, groups - EARLY_GROUPS), others], send_sems.at[1])
+    arrived(early.at[:, :, others], send_sems.at[2])
+    arrived(square_near.at[others], square_sems.at[0])
+    arrived(square_far.at[pl.ds(0, shards_count - 1)], square_sems.at[2])
 
 
 def write_out(*refs):
@@ -406,22 +424,17 @@
             pltpu.VMEM((groups, most, rows, width), jnp.bfloat16),
             pltpu.VMEM((rows, columns), jnp.float32),
             pltpu.VMEM(blocks, jnp.bfloat16),
-            pltpu.VMEM((max(EARLY_GROUPS, 1), replicas, 2, rows, width), jnp.bfloat16),
+            pltpu.VMEM((EARLY_GROUPS, 2, replicas, rows, width), jnp.bfloat16),
             pltpu.VMEM((8, BLOCK), jnp.float32),
             pltpu.VMEM((replicas, 8, BLOCK), jnp.float32),
             pltpu.VMEM((8, BLOCK), jnp.float32),
             pltpu.VMEM((shards_count, 8, BLOCK), jnp.float32),
             dma((replicas + 1, 2)),
-            dma((groups, replicas)),
-            dma((groups, replicas)),
-            dma((groups, most)),
-            dma((groups, most)),
-            dma((groups, replicas)),
-            dma((groups, replicas)),
-            dma((replicas,)),
-            dma((replicas,)),
-            dma((shards_count,)),
-            dma((shards_count,)),
+            dma((3,)),
+            dma((groups, replicas - 1)),
+            dma((EARLY_GROUPS, 2, replicas - 1)),
+            dma((4,)),
+            pltpu.SemaphoreType.REGULAR((1,)),
         ],
         compiler_params=pltpu.CompilerParams(collective_id=0, has_side_effects=True, vmem_limit_bytes=36 * 2**20),
     )(in_hbm(base_weights), in_hbm(inner_weights), in_hbm(momentum))

time: 53.7 us -> 51.1 us (0.952)
  Pallas kernels: 52.9 us -> 50.4 us
    pallas_call x1, Pallas kernels: 49.8 us -> 47.3 us  [shards(): pl.pallas_call(functools.partial(kernel, dims), out_shape=(pltpu.VMEM(bas...]
where the time goes in v1:
time: 51.1 us; the launch traced here: 51 us
  Pallas kernels  50.4 us (99%)
  between operations  0.64 us (1%)
    pallas_call x1, Pallas kernels, shards(): pl.pallas_call(functools.partial(kernel, dims), out_shape=(pltpu.VMEM(bas...  47.3 us
    pallas_call x1, Pallas kernels, shards(): pl.pallas_call(write_out, out_shape=tuple((jax.ShapeDtypeStruct(part.shap...  3.04 us

profile of v1, /device:TPU:0, one launch (start us, length us, event | category | flops | bytes accessed | tf_op | source)
XLA Modules:
  0.0 51.0 jit_solution(3117904149666985)
XLA Ops:
  0.6 47.3 %shard_map.58 = (f32[1024,1024]{1,0:T(8,128)S(1)}, f32[256,1024]{1,0:T(8,128)S(1)}, bf16[1,1024,1024]{2,1,0:T(8,128)(2,1)S(1)}) custom-call(f32[1024,1024]{1,0:T(8,128)} %base_hbm.1, bf16[1,1024,1024]{2,1,0:T(8,128)(2,1)} %inner_hbm.1, f32[256,1024]{1,0:T(8,128)} %momentum_hbm.1), custom_call_target="tpu_custom_call" | custom-call | tf_op jit(solution)/shard_map/pallas_call | solution.py:409
  48.0 3.0 %shard_map.59 = (f32[1024,1024]{1,0:T(8,128)}, f32[256,1024]{1,0:T(8,128)}, bf16[1,1024,1024]{2,1,0:T(8,128)(2,1)}) custom-call(f32[1024,1024]{1,0:T(8,128)S(1)} %get-tuple-element.6.refs_0_, f32[256,1024]{1,0:T(8,128)S(1)} %get-tuple-element.7.refs_1_, bf16[1,1024,1024]{2,1,0:T(8,128)(2,1)S(1)} %get-tuple-element.8.refs_2_), custom_call_target="tpu_custom_call" | custom-call | tf_op jit(solution)/shard_map/pallas_call | solution.py:441

commit v2 on v1

--- a/solution.py
+++ b/solution.py
@@ -48,12 +48,16 @@
     return side, replicas // side
 
 
+def rounds(count):
+    return max(count - 2, 0).bit_length()
+
+
 def kernel(
     dims,
     base_hbm, inner_hbm, momentum_hbm,
     new_base, new_momentum, new_inner,
     base_v, inner_v, momentum_v, dec, first, second, grad, update, early,
-    square_mine, square_near, square_row, square_far,
+    square_mine, square_all,
     load_sems, send_sems, recv_sems, early_sems, square_sems, entry_sems,
 ):
     replicas, shards_count, rows, columns, groups, total = dims
@@ -81,11 +85,23 @@
     def row_start(index):
         return pl.multiple_of(index * rows, rows)
 
+    def greet(sem, step):
+        @pl.when(row_me >= step)
+        def _():
+            pl.semaphore_signal(sem, inc=1, device_id={"fsdp": row_me - step}, device_id_type=MESH)
+
+        @pl.when(row_me + step < shards_count)
+        def _():
+            pl.semaphore_signal(sem, inc=1, device_id={"fsdp": row_me + step}, device_id_type=MESH)
+
+    def greeters(step):
+        below = jnp.where(row_me >= step, 1, 0)
+        return below + jnp.where(row_me + step < shards_count, 1, 0)
+
     barrier = pltpu.get_barrier_semaphore()
     for step in range(1, replicas):
         pl.semaphore_signal(barrier, inc=1, device_id={"replica": near(step)}, device_id_type=MESH)
-    for step in range(1, shards_count):
-        pl.semaphore_signal(barrier, inc=1, device_id={"fsdp": far(step)}, device_id_type=MESH)
+    greet(barrier, 1)
 
     load_order = [(dx, dy) for dy in reversed(range(span_y)) for dx in reversed(range(span_x))]
     loads = []
@@ -168,9 +184,14 @@
                     await_load(g, dp, dq)
                     encode(g, dp, dq)
                     if not greeted:
-                        pl.semaphore_wait(barrier, replicas - 1 + shards_count - 1)
+                        pl.semaphore_wait(barrier, replicas - 1 + greeters(1))
                         greeted = True
                     copy_one(g, dp, dq).start()
+    for at in range(rounds(shards_count)):
+        greet(entry_sems.at[at], 1 << at)
+        pl.semaphore_wait(entry_sems.at[at], greeters(1 << at))
+    for step in range(1, replicas):
+        pl.semaphore_signal(entry_sems.at[rounds(shards_count)], inc=1, device_id={"replica": near(step)}, device_id_type=MESH)
     for dq in reversed(range(most)):
         for g in range(groups):
             if dq < spans(g)[1]:
@@ -237,7 +258,7 @@
             at = pl.ds(pl.multiple_of(t * tile, tile), tile)
             early[g, 1, 0, at] = momentum_v[at, pl.ds(g * width, width)].astype(jnp.bfloat16)
 
-    ahead = (1,)
+    ahead = (1, 0)
     squares = jnp.zeros((8, BLOCK), jnp.float32)
     for g in range(EARLY_GROUPS):
         squares = add_group(g, squares)
@@ -246,14 +267,23 @@
     for g in range(EARLY_GROUPS, groups):
         squares = add_group(g, squares)
 
-    square_mine[...] = squares
-    square_near[0] = squares
-    for step in range(1, replicas):
+    spot = row_me * replicas + me
+    square_row = jnp.sum(squares, axis=0, keepdims=True)
+    square_mine[...] = square_row
+    square_all[spot] = square_row
+    pl.semaphore_wait(entry_sems.at[rounds(shards_count)], replicas - 1)
+    def send_square(step, hop):
         pltpu.make_async_remote_copy(
-            src_ref=square_mine, dst_ref=square_near.at[step],
+            src_ref=square_mine, dst_ref=square_all.at[spot],
             send_sem=square_sems.at[0], recv_sem=square_sems.at[1],
-            device_id={"replica": near(step)}, device_id_type=MESH,
+            device_id={"replica": near(step), "fsdp": far(hop)}, device_id_type=MESH,
         ).start()
+
+    for step in reversed(range(replicas)):
+        @pl.loop(0 if step else 1, shards_count)
+        def _(hop):
+            send_square(step, hop)
+
     for g in range(EARLY_GROUPS):
         for part in (1, 0):
             if part not in ahead:
@@ -261,19 +291,6 @@
     for g in range(EARLY_GROUPS):
         for part in (1, 0):
             early_second(g, part, 0)
-
-    arrived(square_near.at[pl.ds(1, replicas - 1)], square_sems.at[1])
-    squares = square_near[me]
-    for at in range(1, replicas):
-        squares += square_near[lax.rem(me + replicas - at, replicas)]
-    square_row[...] = squares
-    square_far[0] = squares
-    for step in range(1, shards_count):
-        pltpu.make_async_remote_copy(
-            src_ref=square_row, dst_ref=square_far.at[step],
-            send_sem=square_sems.at[2], recv_sem=square_sems.at[3],
-            device_id={"fsdp": far(step)}, device_id_type=MESH,
-        ).start()
 
     for g in range(EARLY_GROUPS):
         np, nq = spans(g)
@@ -289,10 +306,9 @@
             for dp in range(1, np):
                 copy_all(g, dp, 0, dq).start()
 
-    arrived(square_far.at[pl.ds(1, shards_count - 1)], square_sems.at[3])
-    squares = square_far[row_me]
-    for at in range(1, shards_count):
-        squares += square_far[lax.rem(row_me + shards_count - at, shards_count)]
+    everyone = pl.ds(0, shards_count * replicas - 1)
+    arrived(square_all.at[everyone], square_sems.at[1])
+    squares = jnp.sum(square_all[...], axis=0)
     mean_square = jnp.full((1, BLOCK), jnp.sum(squares), jnp.float32) / total
     clip_factor = jnp.minimum(1.0, clip_rms / jnp.sqrt(mean_square + epsilon))
 
@@ -374,8 +390,7 @@
     arrived(dec.at[:, others], send_sems.at[0])
     arrived(update.at[pl.ds(0, groups - EARLY_GROUPS), others], send_sems.at[1])
     arrived(early.at[:, :, others], send_sems.at[2])
-    arrived(square_near.at[others], square_sems.at[0])
-    arrived(square_far.at[pl.ds(0, shards_count - 1)], square_sems.at[2])
+    arrived(square_all.at[everyone], square_sems.at[0])
 
 
 def write_out(*refs):
@@ -425,16 +440,14 @@
             pltpu.VMEM((rows, columns), jnp.float32),
             pltpu.VMEM(blocks, jnp.bfloat16),
             pltpu.VMEM((EARLY_GROUPS, 2, replicas, rows, width), jnp.bfloat16),
-            pltpu.VMEM((8, BLOCK), jnp.float32),
-            pltpu.VMEM((replicas, 8, BLOCK), jnp.float32),
-            pltpu.VMEM((8, BLOCK), jnp.float32),
-            pltpu.VMEM((shards_count, 8, BLOCK), jnp.float32),
+            pltpu.VMEM((1, BLOCK), jnp.float32),
+            pltpu.VMEM((shards_count * replicas, 1, BLOCK), jnp.float32),
             dma((replicas + 1, 2)),
             dma((3,)),
             dma((groups, replicas - 1)),
             dma((EARLY_GROUPS, 2, replicas - 1)),
-            dma((4,)),
-            pltpu.SemaphoreType.REGULAR((1,)),
+            dma((2,)),
+            pltpu.SemaphoreType.REGULAR((rounds(shards_count) + 1,)),
         ],
         compiler_params=pltpu.CompilerParams(collective_id=0, has_side_effects=True, vmem_limit_bytes=36 * 2**20),
     )(in_hbm(base_weights), in_hbm(inner_weights), in_hbm(momentum))

time: 51.1 us -> 49 us (0.959)
  Pallas kernels: 50.4 us -> 48.2 us
    pallas_call x1, Pallas kernels: 47.3 us -> 45.1 us  [shards(): pl.pallas_call(functools.partial(kernel, dims), out_shape=(pltpu.VMEM(bas...]
where the time goes in v2:
time: 49 us; the launch traced here: 48.8 us
  Pallas kernels  48.2 us (98%)
  between operations  0.64 us (1%)
    pallas_call x1, Pallas kernels, shards(): pl.pallas_call(functools.partial(kernel, dims), out_shape=(pltpu.VMEM(bas...  45.1 us
    pallas_call x1, Pallas kernels, shards(): pl.pallas_call(write_out, out_shape=tuple((jax.ShapeDtypeStruct(part.shap...  3.04 us

profile of v2, /device:TPU:0, one launch (start us, length us, event | category | flops | bytes accessed | tf_op | source)
XLA Modules:
  0.0 48.8 jit_solution(9067472595570479496)
XLA Ops:
  0.6 45.1 %shard_map.58 = (f32[1024,1024]{1,0:T(8,128)S(1)}, f32[256,1024]{1,0:T(8,128)S(1)}, bf16[1,1024,1024]{2,1,0:T(8,128)(2,1)S(1)}) custom-call(f32[1024,1024]{1,0:T(8,128)} %base_hbm.1, bf16[1,1024,1024]{2,1,0:T(8,128)(2,1)} %inner_hbm.1, f32[256,1024]{1,0:T(8,128)} %momentum_hbm.1), custom_call_target="tpu_custom_call" | custom-call | tf_op jit(solution)/shard_map/pallas_call | solution.py:424
  45.8 3.0 %shard_map.59 = (f32[1024,1024]{1,0:T(8,128)}, f32[256,1024]{1,0:T(8,128)}, bf16[1,1024,1024]{2,1,0:T(8,128)(2,1)}) custom-call(f32[1024,1024]{1,0:T(8,128)S(1)} %get-tuple-element.6.refs_0_, f32[256,1024]{1,0:T(8,128)S(1)} %get-tuple-element.7.refs_1_, bf16[1,1024,1024]{2,1,0:T(8,128)(2,1)S(1)} %get-tuple-element.8.refs_2_), custom_call_target="tpu_custom_call" | custom-call | tf_op jit(solution)/shard_map/pallas_call | solution.py:454

commit v3 on v2

--- a/solution.py
+++ b/solution.py
@@ -11,6 +11,7 @@
 HALF_GROUPS = 4
 EARLY_GROUPS = 2
 ENCODE_ROWS = 256
+FIRST_GROUPS = 2
 PLAIN_ROWS = 128
 
 code_limit = 448.0
@@ -99,22 +100,28 @@
         return below + jnp.where(row_me + step < shards_count, 1, 0)
 
     barrier = pltpu.get_barrier_semaphore()
-    for step in range(1, replicas):
-        pl.semaphore_signal(barrier, inc=1, device_id={"replica": near(step)}, device_id_type=MESH)
+    beside = [owner(0, dx, 0) for dx in range(1, span_x)]
+    above = [owner(0, 0, dy) for dy in range(1, span_y)]
+    load_order = [(dx, dy) for dy in reversed(range(span_y)) for dx in reversed(range(span_x))]
+    pieces = []
+    for dx, dy in load_order:
+        cuts = [0, columns] if pieces else [0, FIRST_GROUPS * width, columns]
+        pieces += [((dx, dy), low, high) for low, high in zip(cuts, cuts[1:])]
+
+    def load(at):
+        (dx, dy), low, high = pieces[at]
+        here = pl.ds(row_start(owner(0, dx, dy)), rows)
+        cols = pl.ds(low, high - low)
+        pltpu.make_async_copy(base_hbm.at[here, cols], base_v.at[here, cols], load_sems.at[at]).start()
+        pltpu.make_async_copy(inner_hbm.at[0, here, cols], inner_v.at[here, cols], load_sems.at[at]).start()
+
+    load(0)
+    for peer in beside + above:
+        pl.semaphore_signal(barrier, inc=1, device_id={"replica": peer}, device_id_type=MESH)
     greet(barrier, 1)
-
-    load_order = [(dx, dy) for dy in reversed(range(span_y)) for dx in reversed(range(span_x))]
-    loads = []
-    for at, (dx, dy) in enumerate(load_order):
-        here = pl.ds(row_start(owner(0, dx, dy)), rows)
-        pair = (
-            pltpu.make_async_copy(base_hbm.at[here], base_v.at[here], load_sems.at[at, 0]),
-            pltpu.make_async_copy(inner_hbm.at[0, here], inner_v.at[here], load_sems.at[at, 1]),
-        )
-        for copy in pair:
-            copy.start()
-        loads.append(pair)
-    momentum_load = pltpu.make_async_copy(momentum_hbm, momentum_v, load_sems.at[replicas, 0])
+    for at in range(1, len(pieces)):
+        load(at)
+    momentum_load = pltpu.make_async_copy(momentum_hbm, momentum_v, load_sems.at[replicas + 1])
     momentum_load.start()
 
     def encode(g, dp, dq):
@@ -157,11 +164,11 @@
             device_id={"replica": owner(g, dp, dq)}, device_id_type=MESH,
         )
 
-    def copy_early(g, part, dp, dq, source):
+    def copy_early(g, dp, dq, source):
         slot = arrival(g, dp, dq, source)
         return pltpu.make_async_remote_copy(
-            src_ref=early.at[g, part, source if dp else 0], dst_ref=early.at[g, part, slot],
-            send_sem=send_sems.at[2], recv_sem=early_sems.at[g, part, slot - 1],
+            src_ref=early.at[g, source if dp else 0], dst_ref=early.at[g, slot],
+            send_sem=send_sems.at[2], recv_sem=early_sems.at[g, slot - 1],
             device_id={"replica": owner(g, dp, dq)}, device_id_type=MESH,
         )
 
@@ -169,10 +176,10 @@
 
     def await_load(g, dp, dq):
         key = (dp, dq) if g % 2 == 0 else (dq, dp)
-        if key not in waited:
-            waited.add(key)
-            for copy in loads[load_order.index(key)]:
-                copy.wait()
+        for at, (where, low, high) in enumerate(pieces):
+            if where == key and low <= g * width < high and at not in waited:
+                waited.add(at)
+                arrived(base_v.at[pl.ds(0, rows + rows // 2), pl.ds(0, high - low)], load_sems.at[at])
 
     greeted = False
     most = max(span_x, span_y)
@@ -184,41 +191,60 @@
                     await_load(g, dp, dq)
                     encode(g, dp, dq)
                     if not greeted:
-                        pl.semaphore_wait(barrier, replicas - 1 + greeters(1))
+                        pl.semaphore_wait(barrier, len(beside) + len(above) + greeters(1))
                         greeted = True
                     copy_one(g, dp, dq).start()
-    for at in range(rounds(shards_count)):
-        greet(entry_sems.at[at], 1 << at)
-        pl.semaphore_wait(entry_sems.at[at], greeters(1 << at))
-    for step in range(1, replicas):
-        pl.semaphore_signal(entry_sems.at[rounds(shards_count)], inc=1, device_id={"replica": near(step)}, device_id_type=MESH)
+    def sum_one(g, dq):
+        np, nq = spans(g)
+        for dp in range(1, np):
+            copy_one(g, dp, dq).wait_recv()
+
+        @pl.loop(0, rows // tile)
+        def _(t):
+            at = pl.ds(pl.multiple_of(t * tile, tile), tile)
+            summed = dec[g, dq, at].astype(jnp.float32)
+            for dp in range(1, np):
+                summed += first[g, dp * nq + dq, at].astype(jnp.float32)
+            if dq:
+                dec[g, dq, at] = summed.astype(jnp.bfloat16)
+            else:
+                grad[at, pl.ds(g * width, width)] = summed
+
+        if dq:
+            copy_two(g, dq).start()
+
+    line_rounds = rounds(shards_count)
+
+    def call(at):
+        if at < line_rounds:
+            greet(entry_sems.at[at], 1 << at)
+        else:
+            for peer in (beside, above)[at - line_rounds]:
+                pl.semaphore_signal(entry_sems.at[at], inc=1, device_id={"replica": peer}, device_id_type=MESH)
+
+    def hear(at):
+        count = greeters(1 << at) if at < line_rounds else len((beside, above)[at - line_rounds])
+        pl.semaphore_wait(entry_sems.at[at], count)
+
+    call(0)
+    called = 1
+    done = 0
     for dq in reversed(range(most)):
-        for g in range(groups):
-            if dq < spans(g)[1]:
-                await_load(g, 0, dq)
-                encode(g, 0, dq)
-
-    for dq in reversed(range(most)):
-        for g in range(groups):
-            np, nq = spans(g)
-            if dq >= nq:
-                continue
-            for dp in range(1, np):
-                copy_one(g, dp, dq).wait_recv()
-
-            @pl.loop(0, rows // tile)
-            def _(t):
-                at = pl.ds(pl.multiple_of(t * tile, tile), tile)
-                summed = dec[g, dq, at].astype(jnp.float32)
-                for dp in range(1, np):
-                    summed += first[g, dp * nq + dq, at].astype(jnp.float32)
-                if dq:
-                    dec[g, dq, at] = summed.astype(jnp.bfloat16)
-                else:
-                    grad[at, pl.ds(g * width, width)] = summed
-
-            if dq:
-                copy_two(g, dq).start()
+        mine = [g for g in range(groups) if dq < spans(g)[1]]
+        for g in mine:
+            await_load(g, 0, dq)
+            encode(g, 0, dq)
+            done += 1
+            if done % 4 == 0 and called < line_rounds + 2:
+                hear(called - 1)
+                call(called)
+                called += 1
+        for g in mine:
+            sum_one(g, dq)
+    for at in range(called, line_rounds + 2):
+        hear(at - 1)
+        call(at)
+    hear(line_rounds + 1)
 
     def add_group(g, squares):
         nq = spans(g)[1]
@@ -243,27 +269,25 @@
 
         return lax.fori_loop(0, rows // tile, add, squares)
 
-    def early_first(g, part):
+    def early_first(g):
         for dq in range(1, spans(g)[1]):
-            copy_early(g, part, 0, dq, 0).start()
-
-    def early_second(g, part, source):
+            copy_early(g, 0, dq, 0).start()
+
+    def early_second(g, source):
         for dp in range(1, spans(g)[0]):
-            copy_early(g, part, dp, 0, source).start()
+            copy_early(g, dp, 0, source).start()
 
     momentum_load.wait()
     for g in range(EARLY_GROUPS):
         @pl.loop(0, rows // tile)
         def _(t):
             at = pl.ds(pl.multiple_of(t * tile, tile), tile)
-            early[g, 1, 0, at] = momentum_v[at, pl.ds(g * width, width)].astype(jnp.bfloat16)
-
-    ahead = (1, 0)
+            early[g, 0, 1, at] = momentum_v[at, pl.ds(g * width, width)].astype(jnp.bfloat16)
+
     squares = jnp.zeros((8, BLOCK), jnp.float32)
     for g in range(EARLY_GROUPS):
         squares = add_group(g, squares)
-        for part in ahead:
-            early_first(g, part)
+        early_first(g)
     for g in range(EARLY_GROUPS, groups):
         squares = add_group(g, squares)
 
@@ -271,33 +295,30 @@
     square_row = jnp.sum(squares, axis=0, keepdims=True)
     square_mine[...] = square_row
     square_all[spot] = square_row
-    pl.semaphore_wait(entry_sems.at[rounds(shards_count)], replicas - 1)
-    def send_square(step, hop):
+    def send_square(step, row):
         pltpu.make_async_remote_copy(
             src_ref=square_mine, dst_ref=square_all.at[spot],
             send_sem=square_sems.at[0], recv_sem=square_sems.at[1],
-            device_id={"replica": near(step), "fsdp": far(hop)}, device_id_type=MESH,
+            device_id={"replica": near(step), "fsdp": row}, device_id_type=MESH,
         ).start()
 
-    for step in reversed(range(replicas)):
-        @pl.loop(0 if step else 1, shards_count)
-        def _(hop):
-            send_square(step, hop)
+    @pl.loop(0, shards_count - 1)
+    def _(t):
+        at = jnp.where(2 * row_me < shards_count, shards_count - 2 - t, t)
+        row = at + jnp.where(at >= row_me, 1, 0)
+        for step in reversed(range(replicas)):
+            send_square(step, row)
+
+    for step in reversed(range(1, replicas)):
+        send_square(step, row_me)
 
     for g in range(EARLY_GROUPS):
-        for part in (1, 0):
-            if part not in ahead:
-                early_first(g, part)
+        early_second(g, 0)
     for g in range(EARLY_GROUPS):
-        for part in (1, 0):
-            early_second(g, part, 0)
-
-    for g in range(EARLY_GROUPS):
-        np, nq = spans(g)
+        nq = spans(g)[1]
         for dq in range(1, nq):
-            for part in (1, 0):
-                copy_early(g, part, 0, (nq - dq) % nq, 0).wait_recv()
-                early_second(g, part, dq)
+            copy_early(g, 0, (nq - dq) % nq, 0).wait_recv()
+            early_second(g, dq)
 
     def pass_on(g):
         np, nq = spans(g)
@@ -349,8 +370,8 @@
                 from_cols = pl.ds(c, BLOCK)
                 if g < EARLY_GROUPS:
                     _, change = moved_and_change(
-                        early[g, 0, slot, to, from_cols].astype(jnp.float32),
-                        early[g, 1, slot, to, from_cols].astype(jnp.float32),
+                        early[g, slot, 0, to, from_cols].astype(jnp.float32),
+                        early[g, slot, 1, to, from_cols].astype(jnp.float32),
                     )
                 else:
                     change = update[g, slot, to, from_cols].astype(jnp.float32)
@@ -365,8 +386,7 @@
         np = spans(g)[0]
         for dp in range(1, np):
             if g < EARLY_GROUPS:
-                for part in range(2):
-                    copy_early(g, part, (np - dp) % np, 0, dq).wait_recv()
+                copy_early(g, (np - dp) % np, 0, dq).wait_recv()
             else:
                 copy_all(g, (np - dp) % np, 0, dq).wait_recv()
             finish(g, dp, dq)
@@ -389,7 +409,7 @@
     others = pl.ds(0, replicas - 1)
     arrived(dec.at[:, others], send_sems.at[0])
     arrived(update.at[pl.ds(0, groups - EARLY_GROUPS), others], send_sems.at[1])
-    arrived(early.at[:, :, others], send_sems.at[2])
+    arrived(early.at[:, others], send_sems.at[2])
     arrived(square_all.at[everyone], square_sems.at[0])
 
 
@@ -439,15 +459,15 @@
             pltpu.VMEM((groups, most, rows, width), jnp.bfloat16),
             pltpu.VMEM((rows, columns), jnp.float32),
             pltpu.VMEM(blocks, jnp.bfloat16),
-            pltpu.VMEM((EARLY_GROUPS, 2, replicas, rows, width), jnp.bfloat16),
+            pltpu.VMEM((EARLY_GROUPS, replicas, 2, rows, width), jnp.bfloat16),
             pltpu.VMEM((1, BLOCK), jnp.float32),
             pltpu.VMEM((shards_count * replicas, 1, BLOCK), jnp.float32),
-            dma((replicas + 1, 2)),
+            dma((replicas + 2,)),
             dma((3,)),
             dma((groups, replicas - 1)),
-            dma((EARLY_GROUPS, 2, replicas - 1)),
+            dma((EARLY_GROUPS, replicas - 1)),
             dma((2,)),
-            pltpu.SemaphoreType.REGULAR((rounds(shards_count) + 1,)),
+            pltpu.SemaphoreType.REGULAR((rounds(shards_count) + 2,)),
         ],
         compiler_params=pltpu.CompilerParams(collective_id=0, has_side_effects=True, vmem_limit_bytes=36 * 2**20),
     )(in_hbm(base_weights), in_hbm(inner_weights), in_hbm(momentum))

time: 49 us -> 48.2 us (0.984)
  Pallas kernels: 48.2 us -> 47.5 us
    pallas_call x1, Pallas kernels: 45.1 us -> 44.4 us  [shards(): pl.pallas_call(functools.partial(kernel, dims), out_shape=(pltpu.VMEM(bas...]
where the time goes in v3:
time: 48.2 us; the launch traced here: 48.1 us
  Pallas kernels  47.5 us (99%)
  between operations  0.64 us (1%)
    pallas_call x1, Pallas kernels, shards(): pl.pallas_call(functools.partial(kernel, dims), out_shape=(pltpu.VMEM(bas...  44.4 us
    pallas_call x1, Pallas kernels, shards(): pl.pallas_call(write_out, out_shape=tuple((jax.ShapeDtypeStruct(part.shap...  3.04 us

profile of v3, /device:TPU:0, one launch (start us, length us, event | category | flops | bytes accessed | tf_op | source)
XLA Modules:
  0.0 48.1 jit_solution(12353617829028930423)
XLA Ops:
  0.6 44.4 %shard_map.58 = (f32[1024,1024]{1,0:T(8,128)S(1)}, f32[256,1024]{1,0:T(8,128)S(1)}, bf16[1,1024,1024]{2,1,0:T(8,128)(2,1)S(1)}) custom-call(f32[1024,1024]{1,0:T(8,128)} %base_hbm.1, bf16[1,1024,1024]{2,1,0:T(8,128)(2,1)} %inner_hbm.1, f32[256,1024]{1,0:T(8,128)} %momentum_hbm.1), custom_call_target="tpu_custom_call" | custom-call | tf_op jit(solution)/shard_map/pallas_call | solution.py:444
  45.1 3.0 %shard_map.59 = (f32[1024,1024]{1,0:T(8,128)}, f32[256,1024]{1,0:T(8,128)}, bf16[1,1024,1024]{2,1,0:T(8,128)(2,1)}) custom-call(f32[1024,1024]{1,0:T(8,128)S(1)} %get-tuple-element.6.refs_0_, f32[256,1024]{1,0:T(8,128)S(1)} %get-tuple-element.7.refs_1_, bf16[1,1024,1024]{2,1,0:T(8,128)(2,1)S(1)} %get-tuple-element.8.refs_2_), custom_call_target="tpu_custom_call" | custom-call | tf_op jit(solution)/shard_map/pallas_call | solution.py:474

commit v4 on v3

--- a/solution.py
+++ b/solution.py
@@ -9,7 +9,8 @@
 
 BLOCK = 128
 HALF_GROUPS = 4
-EARLY_GROUPS = 2
+EARLY_GROUPS = 4
+EARLY_SHARE = (18, 32)
 ENCODE_ROWS = 256
 FIRST_GROUPS = 2
 PLAIN_ROWS = 128
@@ -40,6 +41,10 @@
 
 def arrived(blocks, sem):
     pltpu.make_async_copy(blocks, blocks, sem).wait()
+
+
+def early_count(rows):
+    return max(rows * EARLY_SHARE[0] // EARLY_SHARE[1] // 8 * 8, 8)
 
 
 def grid_sides(replicas):
@@ -66,6 +71,7 @@
     span_x, span_y = grid_sides(replicas)
     tile = min(PLAIN_ROWS, rows)
     encode_tile = min(ENCODE_ROWS, rows)
+    early_rows = early_count(rows)
     me = lax.axis_index("replica")
     row_me = lax.axis_index("fsdp")
     me_x, me_y = lax.rem(me, span_x), me // span_x
@@ -118,7 +124,11 @@
     load(0)
     for peer in beside + above:
         pl.semaphore_signal(barrier, inc=1, device_id={"replica": peer}, device_id_type=MESH)
-    greet(barrier, 1)
+
+    @pl.when(row_me + 1 < shards_count)
+    def _():
+        pl.semaphore_signal(barrier, inc=1, device_id={"fsdp": row_me + 1}, device_id_type=MESH)
+
     for at in range(1, len(pieces)):
         load(at)
     momentum_load = pltpu.make_async_copy(momentum_hbm, momentum_v, load_sems.at[replicas + 1])
@@ -137,18 +147,21 @@
                 deltas = base_v[at, cols] - inner_v[at, cols].astype(jnp.float32)
                 dec[g, slot, to, pl.ds(c, BLOCK)] = decoded_deltas(deltas).astype(jnp.bfloat16)
 
+    def pair(g):
+        return g // 4 * 2 + g % 2
+
     def copy_one(g, dp, dq):
         slot = dp * spans(g)[1] + dq
         return pltpu.make_async_remote_copy(
             src_ref=dec.at[g, slot], dst_ref=first.at[g, slot],
-            send_sem=send_sems.at[0], recv_sem=recv_sems.at[g, slot - 1],
+            send_sem=send_sems.at[0], recv_sem=recv_sems.at[pair(g), slot - 1],
             device_id={"replica": owner(g, dp, 0)}, device_id_type=MESH,
         )
 
     def copy_two(g, dq):
         return pltpu.make_async_remote_copy(
             src_ref=dec.at[g, dq], dst_ref=second.at[g, dq],
-            send_sem=send_sems.at[0], recv_sem=recv_sems.at[g, dq - 1],
+            send_sem=send_sems.at[0], recv_sem=recv_sems.at[pair(g), dq - 1],
             device_id={"replica": owner(g, 0, dq)}, device_id_type=MESH,
         )
 
@@ -156,11 +169,17 @@
         np, nq = spans(g)
         return ((np - dp) % np) * nq + (source if dp else (nq - dq) % nq)
 
+    def late_low(g):
+        return early_rows if g < EARLY_GROUPS else 0
+
+    def late_part(g):
+        return pl.ds(late_low(g), rows - late_low(g))
+
     def copy_all(g, dp, dq, source):
         slot = arrival(g, dp, dq, source)
         return pltpu.make_async_remote_copy(
-            src_ref=update.at[g, source if dp else 0], dst_ref=update.at[g, slot],
-            send_sem=send_sems.at[1], recv_sem=recv_sems.at[g, slot - 1],
+            src_ref=update.at[g, source if dp else 0, late_part(g)], dst_ref=update.at[g, slot, late_part(g)],
+            send_sem=send_sems.at[3 if g < EARLY_GROUPS else 1], recv_sem=recv_sems.at[pair(g), slot - 1],
             device_id={"replica": owner(g, dp, dq)}, device_id_type=MESH,
         )
 
@@ -168,7 +187,7 @@
         slot = arrival(g, dp, dq, source)
         return pltpu.make_async_remote_copy(
             src_ref=early.at[g, source if dp else 0], dst_ref=early.at[g, slot],
-            send_sem=send_sems.at[2], recv_sem=early_sems.at[g, slot - 1],
+            send_sem=send_sems.at[2], recv_sem=early_sems.at[pair(g), slot - 1],
             device_id={"replica": owner(g, dp, dq)}, device_id_type=MESH,
         )
 
@@ -191,13 +210,15 @@
                     await_load(g, dp, dq)
                     encode(g, dp, dq)
                     if not greeted:
-                        pl.semaphore_wait(barrier, len(beside) + len(above) + greeters(1))
+                        pl.semaphore_wait(barrier, len(beside) + len(above) + jnp.where(row_me > 0, 1, 0))
                         greeted = True
                     copy_one(g, dp, dq).start()
     def sum_one(g, dq):
         np, nq = spans(g)
-        for dp in range(1, np):
-            copy_one(g, dp, dq).wait_recv()
+        if g % 4 < 2:
+            for dp in range(1, np):
+                slot = dp * nq + dq
+                arrived(first.at[pl.ds(0, 2), slot], recv_sems.at[pair(g), slot - 1])
 
         @pl.loop(0, rows // tile)
         def _(t):
@@ -216,15 +237,25 @@
     line_rounds = rounds(shards_count)
 
     def call(at):
-        if at < line_rounds:
-            greet(entry_sems.at[at], 1 << at)
+        if at == 0:
+            @pl.when(row_me > 0)
+            def _():
+                pl.semaphore_signal(entry_sems.at[0], inc=1, device_id={"fsdp": row_me - 1}, device_id_type=MESH)
+        elif at <= line_rounds:
+            greet(entry_sems.at[at], 1 << (at - 1))
         else:
-            for peer in (beside, above)[at - line_rounds]:
+            for peer in (beside, above)[at - line_rounds - 1]:
                 pl.semaphore_signal(entry_sems.at[at], inc=1, device_id={"replica": peer}, device_id_type=MESH)
 
     def hear(at):
-        count = greeters(1 << at) if at < line_rounds else len((beside, above)[at - line_rounds])
-        pl.semaphore_wait(entry_sems.at[at], count)
+        if at == 0:
+            @pl.when(row_me + 1 < shards_count)
+            def _():
+                pl.semaphore_wait(entry_sems.at[0], 1)
+        elif at <= line_rounds:
+            pl.semaphore_wait(entry_sems.at[at], greeters(1 << (at - 1)))
+        else:
+            pl.semaphore_wait(entry_sems.at[at], len((beside, above)[at - line_rounds - 1]))
 
     call(0)
     called = 1
@@ -235,21 +266,22 @@
             await_load(g, 0, dq)
             encode(g, 0, dq)
             done += 1
-            if done % 4 == 0 and called < line_rounds + 2:
+            if done % 3 == 0 and called < line_rounds + 3:
                 hear(called - 1)
                 call(called)
                 called += 1
         for g in mine:
             sum_one(g, dq)
-    for at in range(called, line_rounds + 2):
+    for at in range(called, line_rounds + 3):
         hear(at - 1)
         call(at)
-    hear(line_rounds + 1)
+    hear(line_rounds + 2)
 
     def add_group(g, squares):
         nq = spans(g)[1]
-        for dq in range(1, nq):
-            copy_two(g, dq).wait_recv()
+        if g % 4 < 2:
+            for dq in range(1, nq):
+                arrived(second.at[pl.ds(0, 2), dq], recv_sems.at[pair(g), dq - 1])
 
         def add(t, squares):
             at = pl.ds(pl.multiple_of(t * tile, tile), tile)
@@ -260,8 +292,6 @@
                     summed += second[g, dq, at, pl.ds(c, BLOCK)].astype(jnp.float32)
                 outer = summed * (1.0 / replicas)
                 grad[at, cols] = outer
-                if g < EARLY_GROUPS:
-                    early[g, 0, 0, at, pl.ds(c, BLOCK)] = outer.astype(jnp.bfloat16)
                 square = outer * outer
                 for s in range(0, tile, 8):
                     squares += square[s : s + 8]
@@ -279,14 +309,12 @@
 
     momentum_load.wait()
     for g in range(EARLY_GROUPS):
-        @pl.loop(0, rows // tile)
-        def _(t):
-            at = pl.ds(pl.multiple_of(t * tile, tile), tile)
-            early[g, 0, 1, at] = momentum_v[at, pl.ds(g * width, width)].astype(jnp.bfloat16)
+        early[g, 0, 1] = momentum_v[pl.ds(0, early_rows), pl.ds(g * width, width)].astype(jnp.bfloat16)
 
     squares = jnp.zeros((8, BLOCK), jnp.float32)
     for g in range(EARLY_GROUPS):
         squares = add_group(g, squares)
+        early[g, 0, 0] = grad[pl.ds(0, early_rows), pl.ds(g * width, width)].astype(jnp.bfloat16)
         early_first(g)
     for g in range(EARLY_GROUPS, groups):
         squares = add_group(g, squares)
@@ -314,23 +342,35 @@
 
     for g in range(EARLY_GROUPS):
         early_second(g, 0)
-    for g in range(EARLY_GROUPS):
-        nq = spans(g)[1]
+    early_sets = [(g, g + 2) for g in range(EARLY_GROUPS) if g % 4 < 2]
+
+    def await_early(members, slot):
+        arrived(early.at[pl.ds(0, 2), 0], early_sems.at[pair(members[0]), slot - 1])
+
+    for members in early_sets:
+        for dq in range(1, spans(members[0])[1]):
+            await_early(members, dq)
+            for g in members:
+                early_second(g, dq)
+
+    late_sets = [(g, g + 2) for g in [*range(EARLY_GROUPS, groups), *range(EARLY_GROUPS)] if g % 4 < 2]
+    late = [*range(EARLY_GROUPS, groups), *range(EARLY_GROUPS)]
+
+    def await_late(members, slot):
+        arrived(update.at[pl.ds(0, 2), 0, late_part(members[0])], recv_sems.at[pair(members[0]), slot - 1])
+
+    def pass_on(members):
+        np, nq = spans(members[0])
         for dq in range(1, nq):
-            copy_early(g, 0, (nq - dq) % nq, 0).wait_recv()
-            early_second(g, dq)
-
-    def pass_on(g):
-        np, nq = spans(g)
-        for dq in range(1, nq):
-            copy_all(g, 0, (nq - dq) % nq, 0).wait_recv()
-            for dp in range(1, np):
-                copy_all(g, dp, 0, dq).start()
+            await_late(members, dq)
+            for g in members:
+                for dp in range(1, np):
+                    copy_all(g, dp, 0, dq).start()
 
     everyone = pl.ds(0, shards_count * replicas - 1)
     arrived(square_all.at[everyone], square_sems.at[1])
     squares = jnp.sum(square_all[...], axis=0)
-    mean_square = jnp.full((1, BLOCK), jnp.sum(squares), jnp.float32) / total
+    mean_square = jnp.broadcast_to(jnp.sum(squares, axis=1, keepdims=True), (1, BLOCK)) / total
     clip_factor = jnp.minimum(1.0, clip_rms / jnp.sqrt(mean_square + epsilon))
 
     def moved_and_change(outer, kept):
@@ -338,43 +378,31 @@
         moved = outer_momentum * kept + step_term
         return moved, step_term + outer_momentum * moved
 
-    def advance(g):
-        @pl.loop(0, rows // tile)
-        def _(t):
-            at = pl.ds(pl.multiple_of(t * tile, tile), tile)
+    def advance(g, low, high, sends):
+        for at in range(low, high, tile):
+            part = pl.ds(at, min(tile, high - at))
             for c in range(0, width, BLOCK):
                 cols = pl.ds(g * width + c, BLOCK)
-                moved, change = moved_and_change(grad[at, cols], momentum_v[at, cols])
-                new_momentum[at, cols] = moved
-                if g >= EARLY_GROUPS:
-                    update[g, 0, at, pl.ds(c, BLOCK)] = change.astype(jnp.bfloat16)
-
-    for g in range(EARLY_GROUPS, groups):
-        advance(g)
+                moved, change = moved_and_change(grad[part, cols], momentum_v[part, cols])
+                new_momentum[part, cols] = moved
+                if sends:
+                    update[g, 0, part, pl.ds(c, BLOCK)] = change.astype(jnp.bfloat16)
+
+    for g in late:
+        advance(g, late_low(g), rows, True)
         for dq in range(1, spans(g)[1]):
             copy_all(g, 0, dq, 0).start()
-    for g in range(EARLY_GROUPS, groups):
+    for g in late:
         for dp in range(1, spans(g)[0]):
             copy_all(g, dp, 0, 0).start()
 
-    def finish(g, dp, dq):
-        slot = dp * spans(g)[1] + dq
-        start = row_start(owner(g, dp, dq))
-
-        @pl.loop(0, rows // tile)
-        def _(t):
-            at = pl.ds(pl.multiple_of(start + t * tile, tile), tile)
-            to = pl.ds(pl.multiple_of(t * tile, tile), tile)
+    def finish(g, slot, start, low, high, change_at):
+        def block(part_low, size):
+            at = pl.ds(pl.multiple_of(start + part_low, 8), size)
+            to = pl.ds(part_low, size)
             for c in range(0, width, BLOCK):
                 cols = pl.ds(g * width + c, BLOCK)
-                from_cols = pl.ds(c, BLOCK)
-                if g < EARLY_GROUPS:
-                    _, change = moved_and_change(
-                        early[g, slot, 0, to, from_cols].astype(jnp.float32),
-                        early[g, slot, 1, to, from_cols].astype(jnp.float32),
-                    )
-                else:
-                    change = update[g, slot, to, from_cols].astype(jnp.float32)
+                change = change_at(g, slot, to, pl.ds(c, BLOCK))
                 fresh = base_v[at, cols] - outer_rate * change
                 new_base[at, cols] = fresh
                 blended = blend_share * inner_v[at, cols].astype(jnp.float32) + (
@@ -382,33 +410,55 @@
                 ) * fresh
                 new_inner[0, at, cols] = blended.astype(jnp.bfloat16)
 
-    def finish_last(g, dq):
-        np = spans(g)[0]
-        for dp in range(1, np):
-            if g < EARLY_GROUPS:
-                copy_early(g, (np - dp) % np, 0, dq).wait_recv()
-            else:
-                copy_all(g, (np - dp) % np, 0, dq).wait_recv()
-            finish(g, dp, dq)
+        for at in range(low, high, tile):
+            block(at, min(tile, high - at))
+
+    def early_change(g, slot, to, cols):
+        _, change = moved_and_change(
+            early[g, slot, 0, to, cols].astype(jnp.float32),
+            early[g, slot, 1, to, cols].astype(jnp.float32),
+        )
+        return change
+
+    def late_change(g, slot, to, cols):
+        return update[g, slot, to, cols].astype(jnp.float32)
+
+    def finish_early(g, dp, dq):
+        slot = dp * spans(g)[1] + dq
+        finish(g, slot, row_start(owner(g, dp, dq)), 0, early_rows, early_change)
+
+    def finish_late(g, dp, dq):
+        slot = dp * spans(g)[1] + dq
+        finish(g, slot, row_start(owner(g, dp, dq)), late_low(g), rows, late_change)
 
     for g in range(EARLY_GROUPS):
-        advance(g)
+        advance(g, 0, early_rows, False)
         for dq in range(spans(g)[1]):
-            finish(g, 0, dq)
-    for g in range(EARLY_GROUPS, groups):
-        finish(g, 0, 0)
-    for g in range(EARLY_GROUPS, groups):
-        pass_on(g)
-    for g in range(EARLY_GROUPS, groups):
+            finish_early(g, 0, dq)
+    for g in late:
+        finish_late(g, 0, 0)
+    for members in late_sets:
+        pass_on(members)
+    for g in late:
         for dq in range(1, spans(g)[1]):
-            finish(g, 0, dq)
+            finish_late(g, 0, dq)
     for dq in range(most):
-        for g in range(groups):
-            if dq < spans(g)[1]:
-                finish_last(g, dq)
+        for members in early_sets:
+            np, nq = spans(members[0])
+            for dp in range(1, np if dq < nq else 1):
+                await_early(members, dp * nq + dq)
+                for g in members:
+                    finish_early(g, dp, dq)
+        for members in late_sets:
+            np, nq = spans(members[0])
+            for dp in range(1, np if dq < nq else 1):
+                await_late(members, dp * nq + dq)
+                for g in members:
+                    finish_late(g, dp, dq)
     others = pl.ds(0, replicas - 1)
     arrived(dec.at[:, others], send_sems.at[0])
     arrived(update.at[pl.ds(0, groups - EARLY_GROUPS), others], send_sems.at[1])
+    arrived(update.at[pl.ds(0, EARLY_GROUPS), others, late_part(0)], send_sems.at[3])
     arrived(early.at[:, others], send_sems.at[2])
     arrived(square_all.at[everyone], square_sems.at[0])
 
@@ -459,15 +509,15 @@
             pltpu.VMEM((groups, most, rows, width), jnp.bfloat16),
             pltpu.VMEM((rows, columns), jnp.float32),
             pltpu.VMEM(blocks, jnp.bfloat16),
-            pltpu.VMEM((EARLY_GROUPS, replicas, 2, rows, width), jnp.bfloat16),
+            pltpu.VMEM((EARLY_GROUPS, replicas, 2, early_count(rows), width), jnp.bfloat16),
             pltpu.VMEM((1, BLOCK), jnp.float32),
             pltpu.VMEM((shards_count * replicas, 1, BLOCK), jnp.float32),
             dma((replicas + 2,)),
-            dma((3,)),
-            dma((groups, replicas - 1)),
-            dma((EARLY_GROUPS, replicas - 1)),
+            dma((4,)),
+            dma((groups // 2, replicas - 1)),
+            dma((EARLY_GROUPS // 2, replicas - 1)),
             dma((2,)),
-            pltpu.SemaphoreType.REGULAR((rounds(shards_count) + 2,)),
+            pltpu.SemaphoreType.REGULAR((rounds(shards_count) + 3,)),
         ],
         compiler_params=pltpu.CompilerParams(collective_id=0, has_side_effects=True, vmem_limit_bytes=36 * 2**20),
     )(in_hbm(base_weights), in_hbm(inner_weights), in_hbm(momentum))

time: 48.2 us -> 47.9 us (level)
  no operation moved by 1% of the time
where the time goes in v4:
time: 47.9 us; the launch traced here: 47.8 us
  Pallas kernels  47.1 us (98%)
  between operations  0.64 us (1%)
    pallas_call x1, Pallas kernels, shards(): pl.pallas_call(functools.partial(kernel, dims), out_shape=(pltpu.VMEM(bas...  44.1 us
    pallas_call x1, Pallas kernels, shards(): pl.pallas_call(write_out, out_shape=tuple((jax.ShapeDtypeStruct(part.shap...  3.04 us

profile of v4, /device:TPU:0, one launch (start us, length us, event | category | flops | bytes accessed | tf_op | source)
XLA Modules:
  0.0 47.8 jit_solution(2043810080868133328)
XLA Ops:
  0.6 44.1 %shard_map.58 = (f32[1024,1024]{1,0:T(8,128)S(1)}, f32[256,1024]{1,0:T(8,128)S(1)}, bf16[1,1024,1024]{2,1,0:T(8,128)(2,1)S(1)}) custom-call(f32[1024,1024]{1,0:T(8,128)} %base_hbm.1, bf16[1,1024,1024]{2,1,0:T(8,128)(2,1)} %inner_hbm.1, f32[256,1024]{1,0:T(8,128)} %momentum_hbm.1), custom_call_target="tpu_custom_call" | custom-call | tf_op jit(solution)/shard_map/pallas_call | solution.py:494
  44.7 3.0 %shard_map.59 = (f32[1024,1024]{1,0:T(8,128)}, f32[256,1024]{1,0:T(8,128)}, bf16[1,1024,1024]{2,1,0:T(8,128)(2,1)}) custom-call(f32[1024,1024]{1,0:T(8,128)S(1)} %get-tuple-element.6.refs_0_, f32[256,1024]{1,0:T(8,128)S(1)} %get-tuple-element.7.refs_1_, bf16[1,1024,1024]{2,1,0:T(8,128)(2,1)S(1)} %get-tuple-element.8.refs_2_), custom_call_target="tpu_custom_call" | custom-call | tf_op jit(solution)/shard_map/pallas_call | solution.py:524

commit v5 on v4

--- a/solution.py
+++ b/solution.py
@@ -220,19 +220,18 @@
                 slot = dp * nq + dq
                 arrived(first.at[pl.ds(0, 2), slot], recv_sems.at[pair(g), slot - 1])
 
+        if not dq:
+            return
+
         @pl.loop(0, rows // tile)
         def _(t):
             at = pl.ds(pl.multiple_of(t * tile, tile), tile)
             summed = dec[g, dq, at].astype(jnp.float32)
             for dp in range(1, np):
                 summed += first[g, dp * nq + dq, at].astype(jnp.float32)
-            if dq:
-                dec[g, dq, at] = summed.astype(jnp.bfloat16)
-            else:
-                grad[at, pl.ds(g * width, width)] = summed
-
-        if dq:
-            copy_two(g, dq).start()
+            dec[g, dq, at] = summed.astype(jnp.bfloat16)
+
+        copy_two(g, dq).start()
 
     line_rounds = rounds(shards_count)
 
@@ -278,7 +277,7 @@
     hear(line_rounds + 2)
 
     def add_group(g, squares):
-        nq = spans(g)[1]
+        np, nq = spans(g)
         if g % 4 < 2:
             for dq in range(1, nq):
                 arrived(second.at[pl.ds(0, 2), dq], recv_sems.at[pair(g), dq - 1])
@@ -287,7 +286,9 @@
             at = pl.ds(pl.multiple_of(t * tile, tile), tile)
             for c in range(0, width, BLOCK):
                 cols = pl.ds(g * width + c, BLOCK)
-                summed = grad[at, cols]
+                summed = dec[g, 0, at, pl.ds(c, BLOCK)].astype(jnp.float32)
+                for dp in range(1, np):
+                    summed += first[g, dp * nq, at, pl.ds(c, BLOCK)].astype(jnp.float32)
                 for dq in range(1, nq):
                     summed += second[g, dq, at, pl.ds(c, BLOCK)].astype(jnp.float32)
                 outer = summed * (1.0 / replicas)
@@ -384,9 +385,10 @@
             for c in range(0, width, BLOCK):
                 cols = pl.ds(g * width + c, BLOCK)
                 moved, change = moved_and_change(grad[part, cols], momentum_v[part, cols])
-                new_momentum[part, cols] = moved
                 if sends:
                     update[g, 0, part, pl.ds(c, BLOCK)] = change.astype(jnp.bfloat16)
+                else:
+                    new_momentum[part, cols] = moved
 
     for g in late:
         advance(g, late_low(g), rows, True)
@@ -432,11 +434,11 @@
         finish(g, slot, row_start(owner(g, dp, dq)), late_low(g), rows, late_change)
 
     for g in range(EARLY_GROUPS):
-        advance(g, 0, early_rows, False)
         for dq in range(spans(g)[1]):
             finish_early(g, 0, dq)
     for g in late:
         finish_late(g, 0, 0)
+        advance(g, 0, rows, False)
     for members in late_sets:
         pass_on(members)
     for g in late:

time: 47.9 us -> 47.9 us (level)
  no operation moved by 1% of the time
where the time goes in v5:
time: 47.9 us; the launch traced here: 47.8 us
  Pallas kernels  47.1 us (98%)
  between operations  0.64 us (1%)
    pallas_call x1, Pallas kernels, shards(): pl.pallas_call(functools.partial(kernel, dims), out_shape=(pltpu.VMEM(bas...  44.1 us
    pallas_call x1, Pallas kernels, shards(): pl.pallas_call(write_out, out_shape=tuple((jax.ShapeDtypeStruct(part.shap...  3.04 us

profile of v5, /device:TPU:0, one launch (start us, length us, event | category | flops | bytes accessed | tf_op | source)
XLA Modules:
  0.0 47.8 jit_solution(15782784515647966380)
XLA Ops:
  0.6 44.1 %shard_map.58 = (f32[1024,1024]{1,0:T(8,128)S(1)}, f32[256,1024]{1,0:T(8,128)S(1)}, bf16[1,1024,1024]{2,1,0:T(8,128)(2,1)S(1)}) custom-call(f32[1024,1024]{1,0:T(8,128)} %base_hbm.1, bf16[1,1024,1024]{2,1,0:T(8,128)(2,1)} %inner_hbm.1, f32[256,1024]{1,0:T(8,128)} %momentum_hbm.1), custom_call_target="tpu_custom_call" | custom-call | tf_op jit(solution)/shard_map/pallas_call | solution.py:496
  44.7 3.0 %shard_map.59 = (f32[1024,1024]{1,0:T(8,128)}, f32[256,1024]{1,0:T(8,128)}, bf16[1,1024,1024]{2,1,0:T(8,128)(2,1)}) custom-call(f32[1024,1024]{1,0:T(8,128)S(1)} %get-tuple-element.6.refs_0_, f32[256,1024]{1,0:T(8,128)S(1)} %get-tuple-element.7.refs_1_, bf16[1,1024,1024]{2,1,0:T(8,128)(2,1)S(1)} %get-tuple-element.8.refs_2_), custom_call_target="tpu_custom_call" | custom-call | tf_op jit(solution)/shard_map/pallas_call | solution.py:526
